TPU v7x, 32 devices: a whole 2x2x4 slice. The times are simulated.
32 devices in a mesh: row: 4 (over x, core), col: 8 (over z, y).
Axes of the slice: x: 2, y: 2, z: 4, core: 2. Of those that a mesh axis runs over, the one named last changes fastest.
Arguments:
- adjacency: bfloat16 [4096, 65536], P('row', 'col'), may hold values from -0.03125 to 0.03125
- tile_mask: int32 [16, 256], P('row', 'col'), may hold values from 0 to 1, as said below
- operand: bfloat16 [65536, 1024], P('col'), may hold values from -6 to 6
- current: bfloat16 [4096, 1024], P('row', 'col'), may hold values from 0 to 1
Outputs:
- reached: bfloat16 [4096, 1024], P('row', 'col')
- progress: float32 [16], P('row')
Inputs may be any that keep to these rules, and one draw needn't show every extreme that they name: Split tile_mask into blocks of 4 tile rows by 32 tile columns, aligned to multiples of these. Every block holds at least one nonzero tile, and a block together with the block in the same tile columns whose tile rows start 32 tile rows farther down (upper half of the slab paired with lower half, in order) holds exactly 128 nonzero tiles.
All inputs are finite; a program needn't handle non-finite values.
Results may differ from a plain program's by a relative error of at most 0.0045.
Values may be sent and summed in bfloat16 or wider, within the bound.
A program may use at most 128 MiB of HBM per device.

v0:
```python
import jax
import jax.numpy as jnp
from jax import lax
from jax.sharding import PartitionSpec as P

TILE = 256


def prefix(shard, axis, combine, identity):
    size, mine = (lax.axis_size(axis), lax.axis_index(axis))
    everything = lax.all_gather(shard, axis)
    start = jnp.broadcast_to(jnp.asarray(identity, shard.dtype), shard.shape)

    def turn(k, before):
        reached = k < mine
        new = combine(before, everything[k])
        return jnp.where(reached, new, before)

    return lax.fori_loop(0, size, turn, start)


def add_pair(earlier, later):
    return earlier + later


def local(adjacency, tile_mask, operand, current):
    row_count, col_count = adjacency.shape
    tiles_rows = row_count // TILE
    tiles_cols = col_count // TILE
    keep_tile = tile_mask.astype(jnp.bfloat16)[:, None, :, None]
    masked = (adjacency.reshape(tiles_rows, TILE, tiles_cols, TILE) * keep_tile).reshape(
        row_count, col_count
    )
    partial_value = jnp.dot(masked, operand, preferred_element_type=jnp.float32)
    own_width = current.shape[1]
    logits = lax.psum_scatter(
        partial_value.astype(jnp.bfloat16), "col", scatter_dimension=1, tiled=True
    ).astype(jnp.float32)
    prior_value = current.astype(jnp.float32)
    lifted = (1.0 - prior_value) * jax.nn.sigmoid(logits)
    reached = (prior_value + lifted).astype(jnp.bfloat16)
    window = own_width * lax.axis_size("col")
    local_gain = jnp.sum(lifted.reshape(tiles_rows, TILE * own_width), axis=1) / (TILE * window)
    row_gains = lax.psum(local_gain, "col")
    before = prefix(jnp.sum(row_gains), "row", add_pair, jnp.float32(0.0))
    progress = before + jnp.cumsum(row_gains)
    return (reached, progress)


def solution(mesh):
    placed = (P("row", "col"), P("row", "col"), P("col", None), P("row", "col"))
    return jax.shard_map(
        local, mesh=mesh, in_specs=placed, out_specs=(P("row", "col"), P("row")), check_vma=False
    )
```

profile of v0, /device:TPU:0, one launch (start us, length us, event | category | flops | bytes accessed | tf_op | source)
XLA Modules:
  0.0 167.8 jit_solution(5769564568484707457)
XLA Ops:
  7.2 0.0 reduce-scatter.4.cloned.1.call-start
  7.2 0.7 convert_element_type.16
  7.9 2.7 %mul.14 = bf16[4,256,32,256]{3,2,1,0:T(8,128)(2,1)S(1)} broadcast(bf16[4,32]{1,0:T(4,128)(2,1)S(1)} %convert_element_type.16), dimensions={0,2} | broadcast | bytes 16777472 | tf_op jit(solution)/shard_map/mul | solution.py:31
  10.6 13.9 %copy.8 = bf16[128,8,32,256]{3,1,2,0:T(8,128)(2,1)} copy(bf16[128,8,32,256]{3,2,1,0:T(8,128)(2,1)S(1)} %bitcast.14) | data formatting | bytes 33554432
  24.5 0.0 copy-start
  24.5 0.0 copy-start.1
  24.5 26.3 %fusion.2 = bf16[1024,1024]{1,0:T(8,128)(2,1)S(1)} fusion(bf16[8192,1024]{1,0:T(8,128)(2,1)} %param.8, bf16[1024,8192]{1,0:T(8,128)(2,1)} %param.6, bf16[1024,8192]{1,0:T(8,128)(2,1)} %bitcast.15), kind=kOutput, calls=%fused_computation.2 | convolution fusion | flops 17189306368 | bytes 52428800 | tf_op jit(solution)/shard_map/dot_general | solution.py:34
  50.8 2.6 %copy.6 = bf16[1024,1024]{0,1:T(8,128)(2,1)} copy(bf16[1024,1024]{1,0:T(8,128)(2,1)S(1)} %fusion.2) | data formatting | bytes 4194304
  53.4 0.0 reduce-scatter.4.cloned.1.call-update
  53.4 71.7 %reduce-scatter.4.cloned.1.call-done = bf16[128,1024]{1,0:T(8,128)(2,1)} async-done(((bf16[1024,1024]{1,0:T(8,128)(2,1)}), bf16[128,1024]{1,0:T(8,128)(2,1)}) %reduce-scatter.4.cloned.1.call-update) | async-done | bytes 262160
  125.1 1.1 copy.7
  126.2 0.0 copy-done
  126.2 0.9 fusion.7
  127.1 0.1 reduce_sum.27
  127.2 0.0 copy-done.1
  127.2 0.7 dynamic-slice
  127.9 19.1 %psum.7 = f32[4]{0:T(128)S(1)} all-reduce(f32[4]{0:T(128)S(1)} %broadcast_multiply_fusion), channel_id=1, replica_groups=mesh['row'=4,'col'=8] {'col'}, use_global_device_ids=true, to_apply=%region_3.0 | all-reduce | flops 4 | bytes 32 | tf_op jit(solution)/shard_map/psum | solution.py:44
  147.0 0.6 reduce_sum.28
  147.6 1.4 dynamic-update-slice
  149.1 5.6 %all-reduce = f32[4]{0:T(128)S(1)} all-reduce(f32[4]{0:T(128)S(1)} %dynamic-update-slice), channel_id=1, replica_groups=mesh['row'=4,'col'=8] {'row'}, use_global_device_ids=true, to_apply=%add | all-reduce | flops 4 | bytes 32
  154.7 5.5 %while.13 = (s32[]{:T(128)}, f32[]{:T(128)}, s32[]{:T(128)}, f32[4]{0:T(128)S(1)}, s32[]{:T(128)}) while((s32[]{:T(128)}, f32[]{:T(128)}, s32[]{:T(128)}, f32[4]{0:T(128)S(1)}, s32[]{:T(128)}) %tuple.33), condition=%wide.region_6.7_spmd, body=%wide.region_5.6_spmd.sunk | while | flops 5 | bytes 107 | solution.py:19
  154.7 0.7 dynamic_slice.8
  156.1 0.7 dynamic_slice.8
  157.5 0.7 dynamic_slice.8
  158.8 0.7 dynamic_slice.8
  160.2 0.2 reduce-window.9
  160.4 0.5 add_bitcast_fusion
  (3 shorter events, 0.0 us)
Async XLA Ops:
  7.2 117.9 %reduce-scatter.4.cloned.1.call-start = ((), (), s32[]{:S(2)}) async-start(), calls=%async_computation.1 | async-start | bytes 2359296
  24.5 101.7 %copy-start = (bf16[1024,128]{1,0:T(8,128)(2,1)S(1)}, bf16[1024,128]{1,0:T(8,128)(2,1)}, u32[]{:S(2)}) copy-start(bf16[1024,128]{1,0:T(8,128)(2,1)} %param.9) | copy-start | bytes 786436
  24.5 102.7 %copy-start.1 = (u32[32]{0:T(128)S(1)}, u32[32]{0:T(128)}, u32[]{:S(2)}) copy-start(u32[32]{0:T(128)} %constant.40) | copy-start | bytes 388
Sparse Core Ops, SparseCore 0:
  53.5 71.4 reduce-scatter.3
where the time goes:
time: 168 us
  waiting for transfers between devices  71.7 us (43%)
  matrix products  26.3 us (16%)
  local copies, waits for them, and re-layouts  25.1 us (15%)
  blocking collectives  24.7 us (15%)
  between operations  14.1 us (8%)
  other arithmetic  3.01 us (2%)
  loops' own time  2.85 us (2%)
    unnamed x2, waiting for transfers between devices  71.7 us
    dot_general x1, matrix products, local(): partial_value = jnp.dot(masked, operand, preferred_element_type=jnp.float32)  26.3 us
    unnamed x10, local copies, waits for them, and re-layouts  19.7 us
    psum x1, blocking collectives, local(): row_gains = lax.psum(local_gain, 'col')  19.1 us
    unnamed x1, blocking collectives  5.63 us
  transfers between devices with their start and end apart: 1, of which 1 were waited for; matrix products, arithmetic and copies ran while one was open for 0% of the time, Pallas kernels for 0%

commit v1 on v0

v1 whole, which is shorter than its diff:
```python
import functools

import jax
import jax.numpy as jnp
from jax import lax
from jax.experimental import pallas as pl
from jax.experimental.pallas import tpu as pltpu
from jax.sharding import PartitionSpec as P

TILE = 256
MESH = pl.DeviceIdType.MESH


def fast_size(n):
    size = 1
    while n % (size * 2) == 0 and (size * 2) ** 2 <= n:
        size *= 2
    return size


def kernel(
    n_row, n_col, mask_ref, adj_hbm, op_hbm, cur_hbm, out_hbm, prog_ref,
    adj, op, cur, res, own, ysend, yrecv, zsend, zrecv, gains,
    adj_sem, op_sem, cur_sem, res_sem, ysend_sem, yrecv_sem, zsend_sem, zrecv_sem, gsend_sem, grecv_sem,
):
    nb = fast_size(n_col)
    na = n_col // nb
    rows, depth = adj.shape
    chunks = rows // TILE
    tiles = depth // TILE
    width = cur.shape[1]
    row, col = lax.axis_index("row"), lax.axis_index("col")
    a, b = col // nb, lax.rem(col, nb)
    me = row * n_col + col
    n_dev = n_row * n_col

    def rows_of(i):
        return pl.ds(i * TILE if isinstance(i, int) else pl.multiple_of(i * TILE, TILE), TILE)

    def load_adj(i):
        return pltpu.make_async_copy(adj_hbm.at[rows_of(i)], adj.at[rows_of(i)], adj_sem.at[i])

    def load_op(d, e):
        block = lax.rem(a + e, na) * nb + lax.rem(b + d, nb)
        return pltpu.make_async_copy(
            op_hbm.at[:, pl.ds(pl.multiple_of(block * width, width), width)],
            op.at[d, :, pl.ds(e * width, width)],
            op_sem.at[d, e],
        )

    order = list(range(1, nb)) + [0]
    load_adj(0).start()
    for d in order:
        for e in range(na):
            load_op(d, e).start()
        if d == order[0]:
            for i in range(1, chunks):
                load_adj(i).start()
    load_cur = pltpu.make_async_copy(cur_hbm, cur, cur_sem)
    load_cur.start()

    barrier = pltpu.get_barrier_semaphore()

    def greet(k, carry):
        to = lax.rem(me + k, n_dev)
        pl.semaphore_signal(barrier, inc=1, device_id=(to // n_col, lax.rem(to, n_col)), device_id_type=MESH)
        return carry

    lax.fori_loop(1, n_dev, greet, 0)

    def y_copy(d, i):
        return pltpu.make_async_remote_copy(
            src_ref=ysend.at[d - 1, i], dst_ref=yrecv.at[d - 1, i],
            send_sem=ysend_sem.at[d - 1, i], recv_sem=yrecv_sem.at[d - 1, i],
            device_id=(row, a * nb + lax.rem(b + d, nb)), device_id_type=MESH,
        )

    def z_copy(e, i):
        return pltpu.make_async_remote_copy(
            src_ref=zsend.at[e - 1, i], dst_ref=zrecv.at[e - 1, i],
            send_sem=zsend_sem.at[e - 1, i], recv_sem=zrecv_sem.at[e - 1, i],
            device_id=(row, lax.rem(a + e, na) * nb + b), device_id_type=MESH,
        )

    def product(i, d):
        parts = []
        for k in range(tiles):
            keep = jnp.full((1, TILE), mask_ref[i, k].astype(jnp.float32)).astype(jnp.bfloat16)
            parts.append(adj[rows_of(i), pl.ds(k * TILE, TILE)] * keep)
        left = jnp.concatenate(parts, axis=1)
        return jnp.dot(left, op[d], preferred_element_type=jnp.float32)

    def send_z(i):
        for d in range(1, nb):
            y_copy(d, i).wait_recv()
        for e in list(range(1, na)) + [0]:
            span = pl.ds(e * width, width)
            total = own[rows_of(i), span]
            for d in range(1, nb):
                total = total + yrecv[d - 1, i, :, span].astype(jnp.float32)
            if e:
                zsend[e - 1, i] = total.astype(jnp.bfloat16)
                z_copy(e, i).start()
            else:
                own[rows_of(i), span] = total

    lane = lax.broadcasted_iota(jnp.int32, (1, 128), 1)

    def finish(i, mine):
        logits = own[rows_of(i), pl.ds(0, width)]
        for e in range(1, na):
            z_copy(e, i).wait_recv()
            logits = logits + zrecv[e - 1, i].astype(jnp.float32)
        prior = cur[rows_of(i)].astype(jnp.float32)
        lifted = (1.0 - prior) * jax.nn.sigmoid(logits)
        res[rows_of(i)] = (prior + lifted).astype(jnp.bfloat16)
        save(i).start()
        return jnp.where(lane == i, jnp.sum(lifted) / (TILE * width * n_col), mine)

    def save(i):
        return pltpu.make_async_copy(res.at[rows_of(i)], out_hbm.at[rows_of(i)], res_sem.at[i])

    def turn(i, carry):
        load_adj(i).wait()
        for d in order:
            @pl.when(i == 0)
            def _():
                for e in range(na):
                    load_op(d, e).wait()

            if d:
                ysend[d - 1, i] = product(i, d).astype(jnp.bfloat16)

                if d == order[0]:
                    @pl.when(i == 0)
                    def _():
                        pl.semaphore_wait(barrier, n_dev - 1)

                y_copy(d, i).start()
            else:
                own[rows_of(i)] = product(i, d)

        @pl.when(i > 0)
        def _():
            send_z(i - 1)

        return carry

    lax.fori_loop(0, chunks, turn, 0)
    load_cur.wait()
    mine = jnp.zeros((1, 128), jnp.float32)
    mine = lax.fori_loop(0, chunks - 1, finish, mine)
    send_z(chunks - 1)
    mine = finish(chunks - 1, mine)
    gains[me] = mine

    def g_copy(k):
        to = lax.rem(me + k, n_dev)
        return pltpu.make_async_remote_copy(
            src_ref=gains.at[me], dst_ref=gains.at[me],
            send_sem=gsend_sem.at[k], recv_sem=grecv_sem.at[k],
            device_id=(to // n_col, lax.rem(to, n_col)), device_id_type=MESH,
        )

    def g_start(k, carry):
        g_copy(k).start()
        return carry

    def g_wait(k, carry):
        g_copy(k).wait_recv()
        return carry

    def g_sent(k, carry):
        g_copy(k).wait_send()
        return carry

    lax.fori_loop(1, n_dev, g_start, 0)
    for i in range(chunks):
        for d in range(1, nb):
            y_copy(d, i).wait_send()
        for e in range(1, na):
            z_copy(e, i).wait_send()
        save(i).wait()
    lax.fori_loop(1, n_dev, g_wait, 0)
    every = gains[:, 0, :]
    device = lax.broadcasted_iota(jnp.int32, (n_dev, 128), 0)
    place = lax.broadcasted_iota(jnp.int32, (n_dev, 128), 1)
    before = device < row * n_col
    same = device < (row + 1) * n_col
    for i in range(chunks):
        counts = jnp.logical_or(before, jnp.logical_and(same, place <= i))
        prog_ref[i] = jnp.sum(jnp.where(counts, every, 0.0))
    lax.fori_loop(1, n_dev, g_sent, 0)


def local(n_row, n_col, adjacency, tile_mask, operand, current):
    rows, depth = adjacency.shape
    width = current.shape[1]
    chunks = rows // TILE
    nb = fast_size(n_col)
    na = n_col // nb
    n_dev = n_row * n_col
    bf, f32, dma = jnp.bfloat16, jnp.float32, pltpu.SemaphoreType.DMA
    return pl.pallas_call(
        functools.partial(kernel, n_row, n_col),
        out_shape=(
            jax.ShapeDtypeStruct((rows, width), bf),
            jax.ShapeDtypeStruct((chunks,), f32),
        ),
        in_specs=[pl.BlockSpec(memory_space=pltpu.SMEM)] + [pl.BlockSpec(memory_space=pl.ANY)] * 3,
        out_specs=(pl.BlockSpec(memory_space=pl.ANY), pl.BlockSpec(memory_space=pltpu.SMEM)),
        scratch_shapes=[
            pltpu.VMEM((rows, depth), bf),
            pltpu.VMEM((nb, depth, na * width), bf),
            pltpu.VMEM((rows, width), bf),
            pltpu.VMEM((rows, width), bf),
            pltpu.VMEM((rows, na * width), f32),
            pltpu.VMEM((nb - 1, chunks, TILE, na * width), bf),
            pltpu.VMEM((nb - 1, chunks, TILE, na * width), bf),
            pltpu.VMEM((na - 1, chunks, TILE, width), bf),
            pltpu.VMEM((na - 1, chunks, TILE, width), bf),
            pltpu.VMEM((n_dev, 1, 128), f32),
            dma((chunks,)), dma((nb, na)), dma, dma((chunks,)),
            dma((nb - 1, chunks)), dma((nb - 1, chunks)),
            dma((na - 1, chunks)), dma((na - 1, chunks)),
            dma((n_dev,)), dma((n_dev,)),
        ],
        compiler_params=pltpu.CompilerParams(
            collective_id=0, has_side_effects=True, vmem_limit_bytes=60 * 1024 * 1024
        ),
        name="reach",
    )(tile_mask, adjacency, operand, current)


def solution(mesh):
    placed = (P("row", "col"), P("row", "col"), P("col", None), P("row", "col"))
    return jax.shard_map(
        functools.partial(local, mesh.shape["row"], mesh.shape["col"]),
        mesh=mesh, in_specs=placed, out_specs=(P("row", "col"), P("row")), check_vma=False,
    )
```

time: 168 us -> 58.2 us (0.35)
  waiting for transfers between devices: 71.7 us -> 0 us
  Pallas kernels: 0 us -> 54.6 us
  matrix products: 26.3 us -> 0 us
  blocking collectives: 24.7 us -> 0 us
  local copies, waits for them, and re-layouts: 25.1 us -> 2.8 us
  between operations: 14.1 us -> 0.64 us
  other arithmetic: 3.01 us -> 0 us
  loops' own time: 2.85 us -> 0 us
    unnamed x2 -> x0, waiting for transfers between devices: 71.7 us -> none
    pallas_call x0 -> x1, Pallas kernels: none -> 54.6 us  [local(): pl.pallas_call(functools.partial(kernel, n_row, n_col), out_shape=(jax.Sh...]
    dot_general x1 -> x0, matrix products: 26.3 us -> none  [local(): partial_value = jnp.dot(masked, operand, preferred_element_type=jnp.float32)]
    psum x1 -> x0, blocking collectives: 19.1 us -> none  [local(): row_gains = lax.psum(local_gain, 'col')]
    unnamed x10 -> x2, local copies, waits for them, and re-layouts: 19.7 us -> 2.8 us
    unnamed x1 -> x0, blocking collectives: 5.63 us -> none
    another operation x1 -> x0, loops' own time: 2.85 us -> none  [prefix(): return lax.fori_loop(0, size, turn, start)]
    mul x1 -> x0, local copies, waits for them, and re-layouts: 2.73 us -> none  [local(): adjacency.reshape(tiles_rows, TILE, tiles_cols, TILE) * keep_tile]
  transfers between devices with their start and end apart: 1 -> 0, of which waited for: 1 -> 0; matrix products, arithmetic and copies ran while one was open for 0% -> 0% of each run, Pallas kernels for 0% -> 0%
where the time goes in v1:
time: 58.2 us; the launch traced here: 58.1 us
  Pallas kernels  54.6 us (94%)
  local copies, waits for them, and re-layouts  2.8 us (5%)
  between operations  0.64 us (1%)
    pallas_call x1, Pallas kernels, local(): pl.pallas_call(functools.partial(kernel, n_row, n_col), out_shape=(jax.Sh...  54.6 us
    unnamed x2, local copies, waits for them, and re-layouts  2.8 us

profile of v1, /device:TPU:0, one launch (start us, length us, event | category | flops | bytes accessed | tf_op | source)
XLA Modules:
  0.0 58.1 jit_solution(8680675744026731732)
XLA Ops:
  0.6 54.6 %reach.1 = (bf16[1024,128]{1,0:T(8,128)(2,1)}, f32[4]{0:T(128)}) custom-call(s32[4,32]{1,0:T(4,128)} %mask_ref.1, bf16[1024,8192]{1,0:T(8,128)(2,1)} %adj_hbm.1, bf16[8192,1024]{1,0:T(8,128)(2,1)} %op_hbm.1, bf16[1024,128]{1,0:T(8,128)(2,1)} %cur_hbm.1), custom_call_target="tpu_custom_call" | custom-call | tf_op jit(solution)/shard_map/reach/pallas_call | solution.py:204
  55.3 1.7 %copy.8 = bf16[1024,128]{1,0:T(8,128)(2,1)} copy(bf16[1024,128]{1,0:T(8,128)(2,1)} %get-tuple-element.4) | data formatting | bytes 524288
  56.9 1.1 %copy.9 = f32[4]{0:T(128)} copy(f32[4]{0:T(128)} %get-tuple-element.5) | data formatting | bytes 32
